TPU v7x, 32 devices: a whole 2x2x4 slice. The times are simulated.
32 devices in a mesh: seq: 4 (over y, x), blk: 8 (over z, core).
Axes of the slice: x: 2, y: 2, z: 4, core: 2. Of those that a mesh axis runs over, the one named last changes fastest.
Arguments:
- queries: bfloat16 [4, 2048, 2048], P('seq', 'blk'), may hold values from -150 to 150
- keys: bfloat16 [4, 256, 2048], P('seq', 'blk'), may hold values from -6 to 6
- values: bfloat16 [4, 256, 2048], P('seq', 'blk'), may hold values from -6 to 6
- image_index: int32 [4, 2048], P('seq', 'blk'), may hold values from 0 to 3, as said below
- head_gate: float32 [16], replicated, may hold values from 0.3 to 1.5
- out_weight: bfloat16 [2048, 4096], P(None, 'blk'), may hold values from -0.125 to 0.125
Outputs:
- layer_out: bfloat16 [4, 2048, 4096], P('seq', 'blk')
Inputs may be any that keep to these rules, and one draw needn't show every extreme that they name: Along each sequence image_index never falls; each image's run of text tokens is at least 256 long, so one device's tokens meet at most two images.
All inputs are finite; a program needn't handle non-finite values.
Results may differ from a plain program's by a relative error of at most 0.008.
Values may be sent and summed in bfloat16 or wider, within the bound.
No kernel may reach another device: no remote copies, remote signals or barrier semaphores. Data moves between devices by JAX's collectives and lax.ppermute only.
A program may use at most 128 MiB of HBM per device.

v0:
```python
import jax
import jax.numpy as jnp
from jax import lax
from jax.sharding import PartitionSpec as P

IMAGES = 4


def update(state_in, query_heads, images, key_rows, value_rows, image_rows):
    running_max, running_sum, weighted = state_in
    count = key_rows.shape[0]
    heads = query_heads.shape[1]
    head_size = query_heads.shape[2]
    key_heads = key_rows.reshape(count, heads, head_size)
    value_heads = value_rows.reshape(count, heads, head_size)
    scores = jnp.einsum(
        "thd,lhd->thl", query_heads, key_heads, preferred_element_type=jnp.float32
    ) * head_size ** (-0.5)
    latent_image = lax.iota(jnp.int32, count) // image_rows
    allowed = latent_image[None, None, :] <= images[:, None, None]
    new_max = jnp.maximum(running_max, jnp.max(jnp.where(allowed, scores, -1e30), axis=2))
    probs = jnp.exp(jnp.where(allowed, scores - new_max[:, :, None], -1e30))
    new_sum = jnp.sum(probs, axis=2)
    new_weighted = jnp.einsum(
        "thl,lhd->thd", probs.astype(jnp.bfloat16), value_heads, preferred_element_type=jnp.float32
    )
    return (new_max, new_sum, new_weighted)


def per_device(queries, keys, values, image_index, head_gate, out_weight):
    heads = head_gate.shape[0]
    tok_rows = queries.shape[1]
    query_heads = queries[0].reshape(tok_rows, heads, -1)
    head_size = query_heads.shape[2]
    images = image_index[0]
    image_rows = keys.shape[1] * lax.axis_size("blk") // IMAGES
    initial = (
        jnp.full((tok_rows, heads), -1e30, jnp.float32),
        jnp.zeros((tok_rows, heads), jnp.float32),
        jnp.zeros((tok_rows, heads, head_size), jnp.float32),
    )
    key_rows = lax.all_gather(keys, "blk", axis=1, tiled=True)[0]
    value_rows = lax.all_gather(values, "blk", axis=1, tiled=True)[0]
    state = update(initial, query_heads, images, key_rows, value_rows, image_rows)
    running_max, running_sum, weighted = state
    gate_value = jnp.tanh(head_gate)
    attended = weighted / running_sum[:, :, None] * gate_value[None, :, None]
    hidden = attended.reshape(tok_rows, -1).astype(jnp.bfloat16)
    projected = jnp.dot(
        hidden,
        lax.all_gather(out_weight, "blk", axis=1, tiled=True),
        preferred_element_type=jnp.float32,
    )
    return projected.astype(jnp.bfloat16)[None]


def solution(mesh):
    placed = (
        P("seq", "blk", None),
        P("seq", "blk", None),
        P("seq", "blk", None),
        P("seq", "blk"),
        P(),
        P(None, "blk"),
    )
    return jax.shard_map(
        per_device, mesh=mesh, in_specs=placed, out_specs=P("seq", "blk", None), check_vma=False
    )
```

profile of v0, /device:TPU:0, one launch (start us, length us, event | category | flops | bytes accessed | tf_op | source)
XLA Modules:
  0.0 227.8 jit_solution(4018921631297319439)
XLA Ops:
  6.5 0.0 copy-start.1
  6.5 0.0 copy-start
  6.5 0.0 all-gather.4.cloned.1.call-start
  6.5 0.7 all-gather.4.cloned.1.call-update
  7.3 0.0 all-gather.6.cloned.1.call-start
  7.3 0.7 all-gather.6.cloned.1.call-update
  8.0 0.0 all-gather.8.cloned.1.call-start
  8.1 0.7 all-gather.8.cloned.1.call-update
  8.7 1.4 copy.22
  10.2 0.0 copy-done.1
  10.2 0.0 copy-done
  10.2 0.1 broadcast_compare_fusion
  10.4 23.6 %all-gather.4.cloned.1.call-done = bf16[1,256,2048]{2,1,0:T(8,128)(2,1)} async-done(((bf16[1,32,2048]{2,1,0:T(8,128)(2,1)}), bf16[1,256,2048]{2,1,0:T(8,128)(2,1)}) %all-gather.4.cloned.1.call-update) | async-done | bytes 1048592 | tf_op jit(solution)/shard_map/all_gather | solution.py:42
  33.9 1.5 copy.15
  35.4 22.0 %all-gather.6.cloned.1.call-done = bf16[1,256,2048]{2,1,0:T(8,128)(2,1)} async-done(((bf16[1,32,2048]{2,1,0:T(8,128)(2,1)}), bf16[1,256,2048]{2,1,0:T(8,128)(2,1)}) %all-gather.6.cloned.1.call-update) | async-done | bytes 1048592 | tf_op jit(solution)/shard_map/all_gather | solution.py:43
  57.4 1.5 copy.18
  58.9 1.0 fusion.1
  59.9 0.9 fusion.4
  60.8 1.3 fusion.9
  62.1 147.6 %all-gather.8.cloned.1.call-done = bf16[2048,4096]{1,0:T(8,128)(2,1)} async-done(((bf16[2048,512]{1,0:T(8,128)(2,1)}), bf16[2048,4096]{1,0:T(8,128)(2,1)}) %all-gather.8.cloned.1.call-update) | async-done | bytes 16777232 | tf_op jit(solution)/shard_map/all_gather | solution.py:51
  209.7 11.5 %fusion = bf16[1,256,4096]{2,1,0:T(8,128)(2,1)} fusion(bf16[256,2048]{0,1:T(8,128)(2,1)S(1)} %bitcast.37, bf16[2048,4096]{1,0:T(8,128)(2,1)} %all-gather.8.cloned.1.call-done), kind=kOutput, calls=%fused_computation.1 | convolution fusion | flops 4296015872 | bytes 19922944 | tf_op jit(solution)/shard_map/dot_general | solution.py:49
  (3 shorter events, 0.0 us)
Async XLA Ops:
  6.5 3.7 %copy-start.1 = (f32[16]{0:T(128)S(1)}, f32[16]{0:T(128)}, u32[]{:S(2)}) copy-start(f32[16]{0:T(128)} %param.10) | copy-start | bytes 196
  6.5 3.7 %copy-start = (s32[1,256]{1,0:T(1,128)S(1)}, s32[1,256]{1,0:T(1,128)}, u32[]{:S(2)}) copy-start(s32[1,256]{1,0:T(1,128)} %param.9) | copy-start | bytes 3076
  6.5 27.4 %all-gather.4.cloned.1.call-start = ((), (), s32[]{:S(2)}) async-start(), calls=%async_computation | async-start | bytes 1179648 | tf_op jit(solution)/shard_map/all_gather | solution.py:42
  7.3 50.1 %all-gather.6.cloned.1.call-start = ((), (), s32[]{:S(2)}) async-start(), calls=%async_computation.1 | async-start | bytes 1179648 | tf_op jit(solution)/shard_map/all_gather | solution.py:43
  8.0 201.7 %all-gather.8.cloned.1.call-start = ((), (), s32[]{:S(2)}) async-start(), calls=%async_computation.2 | async-start | bytes 18874368 | tf_op jit(solution)/shard_map/all_gather | solution.py:51
Sparse Core Ops, SparseCore 0:
  8.9 24.9 all-gather.3
  35.5 21.8 all-gather.5
  59.0 150.6 all-gather.7
where the time goes:
time: 228 us
  waiting for transfers between devices  195 us (86%)
  matrix products  13.8 us (6%)
  between operations  13.2 us (6%)
  local copies, waits for them, and re-layouts  4.41 us (2%)
    all_gather x1, waiting for transfers between devices, per_device(): lax.all_gather(out_weight, 'blk', axis=1, tiled=True)  148 us
    all_gather x1, waiting for transfers between devices, per_device(): key_rows = lax.all_gather(keys, 'blk', axis=1, tiled=True)[0]  23.6 us
    all_gather x1, waiting for transfers between devices, per_device(): value_rows = lax.all_gather(values, 'blk', axis=1, tiled=True)[0]  22 us
    dot_general x1, matrix products, per_device(): jnp.dot(hidden, lax.all_gather(out_weight, 'blk', axis=1, tiled=True), pr...  11.5 us
  transfers between devices with their start and end apart: 3, of which 3 were waited for; matrix products, arithmetic and copies ran while one was open for 3% of the time, Pallas kernels for 0%

commit v1 on v0

--- a/solution.py
+++ b/solution.py
@@ -4,6 +4,11 @@
 from jax.sharding import PartitionSpec as P
 
 IMAGES = 4
+
+
+def gathered_along(value, axis, dim):
+    parts = lax.all_gather(value, axis)
+    return jnp.concatenate(parts, axis=dim)
 
 
 def update(state_in, query_heads, images, key_rows, value_rows, image_rows):
@@ -47,9 +52,7 @@
     attended = weighted / running_sum[:, :, None] * gate_value[None, :, None]
     hidden = attended.reshape(tok_rows, -1).astype(jnp.bfloat16)
     projected = jnp.dot(
-        hidden,
-        lax.all_gather(out_weight, "blk", axis=1, tiled=True),
-        preferred_element_type=jnp.float32,
+        hidden, gathered_along(out_weight, "blk", 1), preferred_element_type=jnp.float32
     )
     return projected.astype(jnp.bfloat16)[None]
 

time: 228 us -> 257 us (1.13)
  local copies, waits for them, and re-layouts: 4.41 us -> 26 us
  matrix products: 13.8 us -> 20.2 us
    reshape x0 -> x1, local copies, waits for them, and re-layouts: none -> 21.6 us  [gathered_along(): return jnp.concatenate(parts, axis=dim)]
    dot_general x1, matrix products: 11.5 us -> 17.9 us  [per_device(): jnp.dot(hidden, gathered_along(out_weight, 'blk', 1), preferred_element_t...]
where the time goes in v1:
time: 257 us; the launch traced here: 256 us
  waiting for transfers between devices  195 us (76%)
  local copies, waits for them, and re-layouts  26 us (10%)
  matrix products  20.2 us (8%)
  between operations  13.2 us (5%)
    all_gather x1, waiting for transfers between devices, gathered_along(): parts = lax.all_gather(value, axis)  148 us
    all_gather x1, waiting for transfers between devices, per_device(): key_rows = lax.all_gather(keys, 'blk', axis=1, tiled=True)[0]  23.6 us
    all_gather x1, waiting for transfers between devices, per_device(): value_rows = lax.all_gather(values, 'blk', axis=1, tiled=True)[0]  22 us
    reshape x1, local copies, waits for them, and re-layouts, gathered_along(): return jnp.concatenate(parts, axis=dim)  21.6 us
    dot_general x1, matrix products, per_device(): jnp.dot(hidden, gathered_along(out_weight, 'blk', 1), preferred_element_t...  17.9 us
  transfers between devices with their start and end apart: 3, of which 3 were waited for; matrix products, arithmetic and copies ran while one was open for 3% of the time, Pallas kernels for 0%

profile of v1, /device:TPU:0, one launch (start us, length us, event | category | flops | bytes accessed | tf_op | source)
XLA Modules:
  0.0 255.8 jit_solution(10253306595045270157)
XLA Ops:
  6.5 0.0 copy-start.1
  6.5 0.0 copy-start
  6.5 0.0 all-gather.5.cloned.1.call-start
  6.5 0.7 all-gather.5.cloned.1.call-update
  7.3 0.0 all-gather.7.cloned.1.call-start
  7.3 0.7 all-gather.7.cloned.1.call-update
  8.0 0.0 all-gather.9.cloned.1.call-start
  8.1 0.7 all-gather.9.cloned.1.call-update
  8.7 1.4 copy.29
  10.2 0.0 copy-done.1
  10.2 0.0 copy-done
  10.2 0.1 broadcast_compare_fusion
  10.4 23.6 %all-gather.5.cloned.1.call-done = bf16[1,256,2048]{2,1,0:T(8,128)(2,1)} async-done(((bf16[1,32,2048]{2,1,0:T(8,128)(2,1)}), bf16[1,256,2048]{2,1,0:T(8,128)(2,1)}) %all-gather.5.cloned.1.call-update) | async-done | bytes 1048592 | tf_op jit(solution)/shard_map/all_gather | solution.py:47
  33.9 1.5 copy.21
  35.4 22.0 %all-gather.7.cloned.1.call-done = bf16[1,256,2048]{2,1,0:T(8,128)(2,1)} async-done(((bf16[1,32,2048]{2,1,0:T(8,128)(2,1)}), bf16[1,256,2048]{2,1,0:T(8,128)(2,1)}) %all-gather.7.cloned.1.call-update) | async-done | bytes 1048592 | tf_op jit(solution)/shard_map/all_gather | solution.py:48
  57.4 1.5 copy.24
  58.9 1.0 fusion.1
  59.9 0.9 fusion.4
  60.8 1.3 fusion.9
  62.1 147.6 %all-gather.9.cloned.1.call-done = bf16[16384,512]{1,0:T(8,128)(2,1)} async-done(((bf16[2048,512]{1,0:T(8,128)(2,1)}), bf16[16384,512]{1,0:T(8,128)(2,1)}) %all-gather.9.cloned.1.call-update) | async-done | bytes 16777232 | tf_op jit(solution)/shard_map/all_gather | solution.py:10
  209.7 21.6 %copy.26 = bf16[2048,8,512]{0,2,1:T(8,128)(2,1)} copy(bf16[2048,8,512]{2,0,1:T(8,128)(2,1)} %bitcast.39) | data formatting | bytes 33554432 | tf_op jit(solution)/shard_map/reshape | solution.py:11
  231.3 17.9 %fusion = bf16[1,256,4096]{2,1,0:T(8,128)(2,1)} fusion(bf16[256,2048]{0,1:T(8,128)(2,1)S(1)} %bitcast.46, bf16[2048,4096]{0,1:T(8,128)(2,1)} %bitcast.40), kind=kOutput, calls=%fused_computation.1 | convolution fusion | flops 4296015872 | bytes 19922944 | tf_op jit(solution)/shard_map/dot_general | solution.py:54
  (3 shorter events, 0.0 us)
Async XLA Ops:
  6.5 3.7 %copy-start.1 = (f32[16]{0:T(128)S(1)}, f32[16]{0:T(128)}, u32[]{:S(2)}) copy-start(f32[16]{0:T(128)} %param.10) | copy-start | bytes 196
  6.5 3.7 %copy-start = (s32[1,256]{1,0:T(1,128)S(1)}, s32[1,256]{1,0:T(1,128)}, u32[]{:S(2)}) copy-start(s32[1,256]{1,0:T(1,128)} %param.9) | copy-start | bytes 3076
  6.5 27.4 %all-gather.5.cloned.1.call-start = ((), (), s32[]{:S(2)}) async-start(), calls=%async_computation | async-start | bytes 1179648 | tf_op jit(solution)/shard_map/all_gather | solution.py:47
  7.3 50.1 %all-gather.7.cloned.1.call-start = ((), (), s32[]{:S(2)}) async-start(), calls=%async_computation.1 | async-start | bytes 1179648 | tf_op jit(solution)/shard_map/all_gather | solution.py:48
  8.0 201.7 %all-gather.9.cloned.1.call-start = ((), (), s32[]{:S(2)}) async-start(), calls=%async_computation.2 | async-start | bytes 18874368 | tf_op jit(solution)/shard_map/all_gather | solution.py:10
Sparse Core Ops, SparseCore 0:
  8.9 24.9 all-gather.4
  35.5 21.8 all-gather.6
  59.0 150.6 all-gather.8
